TPU v7x, 32 devices: a whole 2x2x4 slice. The times are simulated.
32 devices in a mesh: wide: 16 (over z, x, core), pair: 2 (over y).
Axes of the slice: x: 2, y: 2, z: 4, core: 2. Of those that a mesh axis runs over, the one named last changes fastest.
Arguments:
- pooled_b: bfloat16 [32, 16, 512, 128], P('wide', None, 'pair'), may hold values from -6 to 6
- dense_output_second: bfloat16 [8192, 128], P(('wide', 'pair')), may hold values from -4 to 4
- counts_b: int32 [8192, 26], P(('wide', 'pair')), may hold values from 1 to 8
- slot_of: int32 [32], replicated, may hold values from 0 to 31, each once
- stacked_a: bfloat16 [8192, 3456], P(('wide', 'pair')), may hold values from -4 to 4
- upstream_a: bfloat16 [8192, 3456], P(('wide', 'pair')), may hold values from -2 to 2
- counts_a: int32 [8192, 26], P(('wide', 'pair')), may hold values from 1 to 8
- down_projection: bfloat16 [3456, 512], P('wide'), may hold values from -0.109375 to 0.109375
- proj_up: bfloat16 [512, 3456], P(None, 'wide'), may hold values from -0.25 to 0.25
- cross_layer_bias: bfloat16 [3456], P('wide'), may hold values from -3 to 3
Outputs:
- crossed_b: bfloat16 [8192, 3456], P(('wide', 'pair'))
- dense_grad_a: bfloat16 [8192, 128], P(('wide', 'pair'))
- pooled_grad_a: bfloat16 [32, 16, 512, 128], P('wide', None, 'pair')
- grad_down: float32 [3456, 512], P('wide')
- grad_up: float32 [512, 3456], P(None, 'wide')
- grad_bias: float32 [3456], P('wide')
Inputs may be any that keep to these rules, and one draw needn't show every extreme that they name: slot_of holds every slot once; its first 26 entries are the slots of tables 0 to 25, the rest are unused. Slot s lies on index s // 2 of wide.
All inputs are finite; a program needn't handle non-finite values.
Results may differ from a plain program's by a relative error of at most 0.0075.
Values may be sent and summed in bfloat16 or wider, within the bound.
A program may use at most 128 MiB of HBM per device.

v0:
```python
import jax
import jax.numpy as jnp
from jax import lax
from jax.sharding import PartitionSpec as P


def table_means(slot_rows, lookup_count, table_slots):
    picked = jnp.take(slot_rows, table_slots, axis=0).astype(jnp.float32)
    scaled = picked / jnp.transpose(lookup_count).astype(jnp.float32)[:, :, None]
    return jnp.transpose(scaled, (1, 0, 2)).reshape(scaled.shape[1], -1).astype(jnp.bfloat16)


def cross_forward(stacked, down, up):
    low_rank = jnp.dot(stacked, down, preferred_element_type=jnp.float32).astype(jnp.bfloat16)
    projected = jnp.dot(low_rank, up, preferred_element_type=jnp.float32)
    return (low_rank, projected)


def crossed_output(stacked, projected, bias):
    stacked_wide = stacked.astype(jnp.float32)
    return (stacked_wide * (projected + bias.astype(jnp.float32)) + stacked_wide).astype(
        jnp.bfloat16
    )


def cross_backward(stacked, upstream, lookup_count, down, up, bias, feature_index):
    low_rank, projected = cross_forward(stacked, down, up)
    stacked_wide = stacked.astype(jnp.float32)
    upstream_wide = upstream.astype(jnp.float32)
    scale_grad = upstream_wide * stacked_wide
    grad_bias = jnp.sum(scale_grad, axis=0)
    proj_grad = scale_grad.astype(jnp.bfloat16)
    over_rows = (((0,), (0,)), ((), ()))
    over_cols = (((1,), (1,)), ((), ()))
    grad_up = lax.dot_general(low_rank, proj_grad, over_rows, preferred_element_type=jnp.float32)
    low_grad = lax.dot_general(proj_grad, up, over_cols, preferred_element_type=jnp.float32).astype(
        jnp.bfloat16
    )
    grad_down = lax.dot_general(stacked, low_grad, over_rows, preferred_element_type=jnp.float32)
    input_grad = upstream_wide * (projected + bias.astype(jnp.float32)) + upstream_wide
    input_grad = input_grad + lax.dot_general(
        low_grad, down, over_cols, preferred_element_type=jnp.float32
    )
    rows = stacked.shape[0]
    dense_gradient = input_grad[:, :feature_index].astype(jnp.bfloat16)
    table_gradient = (
        input_grad[:, feature_index:].reshape(rows, -1, feature_index)
        / lookup_count.astype(jnp.float32)[:, :, None]
    )
    table_gradient = jnp.transpose(table_gradient, (1, 0, 2)).astype(jnp.bfloat16)
    return (dense_gradient, table_gradient, grad_down, grad_up, grad_bias)


def local(
    pooled_b,
    dense_output_second,
    counts_b,
    slot_of,
    stacked_a,
    upstream_a,
    counts_a,
    down_projection,
    proj_up,
    cross_layer_bias,
):
    feature_index = dense_output_second.shape[1]
    tables = counts_b.shape[1]
    table_slots = slot_of[:tables]
    arrived = lax.all_to_all(pooled_b, "wide", split_axis=1, concat_axis=0, tiled=True)
    slot_count = arrived.shape[0]
    samples = arrived.shape[2]
    down, up, bias = (
        lax.all_gather(down_projection, "wide", axis=0, tiled=True),
        lax.all_gather(proj_up, "wide", axis=1, tiled=True),
        lax.all_gather(cross_layer_bias, "wide", axis=0, tiled=True),
    )
    slot_rows = arrived.reshape(slot_count, samples, feature_index)
    stacked_b = jnp.concatenate(
        [dense_output_second, table_means(slot_rows, counts_b, table_slots)], axis=1
    )
    low_rank, projected = cross_forward(stacked_b, down, up)
    crossed_b = crossed_output(stacked_b, projected, bias)
    dense_gradient, table_gradient, grad_down, grad_up, grad_bias = cross_backward(
        stacked_a, upstream_a, counts_a, down, up, bias, feature_index
    )
    slot_selector = (
        table_slots[None, :] == jnp.arange(slot_count, dtype=jnp.int32)[:, None]
    ).astype(jnp.bfloat16)
    slot_grad = jnp.einsum(
        "qv,vxk->qxk", slot_selector, table_gradient, preferred_element_type=jnp.float32
    ).astype(jnp.bfloat16)
    returned = lax.all_to_all(
        slot_grad.reshape(slot_count, 1, samples, feature_index),
        "wide",
        split_axis=0,
        concat_axis=1,
        tiled=True,
    )
    shares = (
        lax.psum_scatter(grad_down, "wide", scatter_dimension=0, tiled=True),
        lax.psum_scatter(grad_up, "wide", scatter_dimension=1, tiled=True),
        lax.psum_scatter(grad_bias, "wide", scatter_dimension=0, tiled=True),
    )
    summed = (
        lax.psum(shares[0].astype(jnp.bfloat16), "pair").astype(jnp.float32),
        lax.psum(shares[1].astype(jnp.bfloat16), "pair").astype(jnp.float32),
        lax.psum(shares[2].astype(jnp.bfloat16), "pair").astype(jnp.float32),
    )
    return (crossed_b, dense_gradient, returned, summed[0], summed[1], summed[2])


def solution(mesh):
    return jax.shard_map(
        local,
        mesh=mesh,
        in_specs=(
            P("wide", None, "pair", None),
            P(("wide", "pair"), None),
            P(("wide", "pair"), None),
            P(),
            P(("wide", "pair"), None),
            P(("wide", "pair"), None),
            P(("wide", "pair"), None),
            P("wide", None),
            P(None, "wide"),
            P("wide"),
        ),
        out_specs=(
            P(("wide", "pair"), None),
            P(("wide", "pair"), None),
            P("wide", None, "pair", None),
            P("wide", None),
            P(None, "wide"),
            P("wide"),
        ),
        check_vma=False,
    )
```

profile of v0, /device:TPU:0, one launch (start us, length us, event | category | flops | bytes accessed | tf_op | source)
XLA Modules:
  0.0 427.8 jit_solution(16351802026620585940)
XLA Ops:
  7.2 0.0 all-gather.5.cloned.1.call-start
  7.2 0.7 all-gather.5.cloned.1.call-update
  7.9 0.0 all-gather.3.cloned.1.call-start
  7.9 0.7 all-gather.3.cloned.1.call-update
  8.7 0.0 reduce-scatter.7.cloned.1.call-start
  8.7 51.4 %all-gather.5.cloned.1.call-done = bf16[512,3456]{0,1:T(8,128)(2,1)} async-done(((bf16[512,216]{0,1:T(8,128)(2,1)}), bf16[512,3456]{0,1:T(8,128)(2,1)}) %all-gather.5.cloned.1.call-update) | async-done | bytes 3538960 | tf_op jit(solution)/shard_map/all_gather | solution.py:74
  60.1 4.2 convolution_convert_fusion
  64.3 0.0 copy-start.4
  64.3 0.7 copy-done.4
  65.0 4.1 convolution_bitcast_fusion
  69.1 8.1 %copy.35 = f32[3456,512]{1,0:T(8,128)} copy(f32[3456,512]{0,1:T(8,128)} %convolution_bitcast_fusion) | data formatting | bytes 14155776
  77.2 0.0 reduce-scatter.7.cloned.1.call-update
  77.2 0.0 copy-start.1
  77.2 0.0 reduce-scatter.5.cloned.1.call-start
  77.3 30.9 %all-gather.3.cloned.1.call-done = bf16[3456,512]{1,0:T(8,128)(2,1)} async-done(((bf16[216,512]{1,0:T(8,128)(2,1)}), bf16[3456,512]{1,0:T(8,128)(2,1)}) %all-gather.3.cloned.1.call-update) | async-done | bytes 3538960 | tf_op jit(solution)/shard_map/all_gather | solution.py:73
  108.2 3.1 convolution_convert_fusion.1
  111.3 0.0 copy-start.6
  111.3 0.7 copy-done.6
  112.0 4.1 fusion.9
  116.1 0.0 reduce-scatter.5.cloned.1.call-update
  116.1 0.0 copy-start.8
  116.1 0.0 copy-start.10
  116.1 3.2 copy.27
  119.3 4.5 %all-to-all-start = ((bf16[2,16,256,128]{3,2,0,1:T(8,128)(2,1)}), bf16[2,16,256,128]{3,2,0,1:T(8,128)(2,1)}, u32[]{:S(2)}, u32[]{:S(2)}) async-start(bf16[2,16,256,128]{3,2,0,1:T(8,128)(2,1)} %copy.27), calls=%async_computation | async-start | bytes 4194304 | tf_op jit(solution)/shard_map/all_to_all | solution.py:69
  123.8 0.6 fusion.17
  125.0 0.2 dynamic-update-slice
  125.3 79.6 %all-reduce = bf16[3456]{0:T(1024)(128)(2,1)} all-reduce(bf16[3456]{0:T(1024)(128)(2,1)S(1)} %dynamic-update-slice), channel_id=1, replica_groups=mesh['wide'=16,'pair'=2] {'wide'}, use_global_device_ids=true, to_apply=%add | all-reduce | flops 3456 | bytes 13824
  204.9 0.7 convert_element_type.84
  205.6 1.4 convert_element_type.91
  206.9 3.4 fusion.1
  210.3 1.1 convolution_add_fusion
  211.5 1.7 copy-done.2
  213.3 2.1 slice.16
  215.3 5.0 %copy.30 = f32[256,3328]{0,1:T(8,128)} copy(f32[256,3328]{1,0:T(8,128)} %slice.16) | data formatting | bytes 6815744 | tf_op jit(solution)/shard_map/slice | solution.py:47
  220.4 3.6 fusion.8
  223.9 4.5 %copy.31 = bf16[26,256,128]{2,0,1:T(8,128)(2,1)} copy(bf16[26,256,128]{1,2,0:T(8,128)(2,1)} %fusion.8) | data formatting | bytes 3407872 | tf_op jit(solution)/shard_map/convert_element_type | solution.py:50
  228.4 2.3 convert_bitcast_fusion
  230.7 2.1 copy.32
  232.8 0.0 all-to-all-done
  232.8 22.1 %all-to-all-start.1 = ((bf16[32,1,256,128]{3,2,1,0:T(8,128)(2,1)}), bf16[32,1,256,128]{3,2,1,0:T(8,128)(2,1)}, u32[]{:S(2)}, u32[]{:S(2)}) async-start(bf16[32,1,256,128]{3,2,1,0:T(8,128)(2,1)} %copy.32), calls=%async_computation.1 | async-start | bytes 4194304 | tf_op jit(solution)/shard_map/all_to_all | solution.py:92
  254.9 0.0 all-reduce.5.cloned.1.call-start
  255.0 1.4 convert_element_type.79
  257.0 1.1 fusion.6
  258.1 115.6 %all-reduce.1 = bf16[3456]{0:T(1024)(128)(2,1)S(1)} all-reduce(f32[3456]{0:T(1024)} %fusion.6), channel_id=4, replica_groups=mesh['wide'=16,'pair'=2] {'wide'}, use_global_device_ids=true, to_apply=%region_5.6.clone | all-reduce | flops 3456 | bytes 20736
  373.8 0.1 dynamic-slice.4
  373.8 5.1 %psum.23 = bf16[216]{0:T(256)(128)(2,1)S(1)} all-reduce(bf16[216]{0:T(256)(128)(2,1)S(1)} %dynamic-slice.4), channel_id=1, replica_groups=mesh['wide'=16,'pair'=2] {'pair'}, use_global_device_ids=true, to_apply=%region_6.7 | all-reduce | flops 216 | bytes 864 | tf_op jit(solution)/shard_map/psum | solution.py:107
  378.9 0.6 convert_element_type.100
  379.5 0.7 compare_and_fusion
  380.2 2.5 gather_fusion
  382.6 0.0 copy-done.7
  382.6 1.2 fusion.5
  383.8 1.8 copy.28
  385.6 0.0 copy-start.9
  385.6 1.3 copy.29
  386.9 1.5 slice.19
  388.4 1.9 copy.36
  390.3 1.7 convert_element_type.97
  392.0 0.0 all-reduce.5.cloned.1.call-update
  392.1 6.6 %fusion.4 = bf16[256,3456]{1,0:T(8,128)(2,1)} fusion(bf16[512,3456]{0,1:T(8,128)(2,1)} %all-gather.5.cloned.1.call-done, f32[3456]{0:T(1024)S(1)} %convert_element_type.84, bf16[256,3328]{1,0:T(8,128)(2,1)S(1)} %copy.29, bf16[256,128]{1,0:T(8,128)(2,1)S(1)} %copy-done.9, bf16[3456,512]{1,0:T(8,128)(2,1)} %all-gather.3.cloned.1.call-done), kind=kOutput, calls=%fused_computation.9 | convolution fusion | flops 1822687232 | bytes 10630656 | tf_op jit(solution)/shard_map/dot_general | solution.py:15
  398.6 0.0 all-to-all-done.1
  398.6 3.1 copy.38
  401.8 15.9 %all-reduce.5.cloned.1.call-done = (bf16[216,512]{0,1:T(8,128)(2,1)}, bf16[512,216]{0,1:T(8,128)(2,1)}) async-done(((bf16[216,512]{0,1:T(8,128)(2,1)}, bf16[512,216]{0,1:T(8,128)(2,1)}), (bf16[216,512]{0,1:T(8,128)(2,1)}, bf16[512,216]{0,1:T(8,128)(2,1)})) %all-reduce.5.cloned.1.call-update) | async-done | bytes 442384 | tf_op jit(solution)/shard_map/psum | solution.py:105
  417.7 1.7 convert_element_type.98
  419.4 1.8 copy.34
  (16 shorter events, 0.0 us)
Async XLA Ops:
  7.2 53.0 %all-gather.5.cloned.1.call-start = ((), (), s32[]{:S(2)}) async-start(), calls=%async_computation.5 | async-start | bytes 3760128 | tf_op jit(solution)/shard_map/all_gather | solution.py:74
  7.9 100.3 %all-gather.3.cloned.1.call-start = ((), (), s32[]{:S(2)}) async-start(), calls=%async_computation.4 | async-start | bytes 3760128 | tf_op jit(solution)/shard_map/all_gather | solution.py:73
  8.6 56.4 %copy-start = (bf16[256,3456]{1,0:T(8,128)(2,1)S(1)}, bf16[256,3456]{1,0:T(8,128)(2,1)}, u32[]{:S(2)}) copy-start(bf16[256,3456]{1,0:T(8,128)(2,1)} %param.14) | copy-start | bytes 5308420
  8.7 379.8 %reduce-scatter.7.cloned.1.call-start = ((), (), s32[]{:S(2)}) async-start(), calls=%async_computation.7 | async-start | bytes 7520256
  64.3 0.7 copy-start.4
  77.2 34.8 %copy-start.1 = (bf16[256,3456]{1,0:T(8,128)(2,1)S(1)}, bf16[256,3456]{1,0:T(8,128)(2,1)}, u32[]{:S(2)}) copy-start(bf16[256,3456]{1,0:T(8,128)(2,1)} %param.15) | copy-start | bytes 5308420
  77.2 313.1 %reduce-scatter.5.cloned.1.call-start = ((), (), s32[]{:S(2)}) async-start(), calls=%async_computation.6 | async-start | bytes 7520256 | tf_op jit(solution)/shard_map/reduce_scatter | solution.py:101
  111.3 0.7 copy-start.6
  116.1 7.7 %copy-start.8 = (u32[32]{0:T(128)S(1)}, u32[32]{0:T(128)}, u32[]{:S(2)}) copy-start(u32[32]{0:T(128)} %constant.24) | copy-start | bytes 388
  116.1 8.9 %copy-start.10 = (bf16[216]{0:T(256)(128)(2,1)S(1)}, bf16[216]{0:T(256)(128)(2,1)}, u32[]{:S(2)}) copy-start(bf16[216]{0:T(256)(128)(2,1)} %param.19) | copy-start | bytes 1300
  119.3 113.5 %all-to-all-start = ((bf16[2,16,256,128]{3,2,0,1:T(8,128)(2,1)}), bf16[2,16,256,128]{3,2,0,1:T(8,128)(2,1)}, u32[]{:S(2)}, u32[]{:S(2)}) async-start(bf16[2,16,256,128]{3,2,0,1:T(8,128)(2,1)} %copy.27), calls=%async_computation | async-start | bytes 4194304 | tf_op jit(solution)/shard_map/all_to_all | solution.py:69
  206.9 3.4 copy-start.3
  206.9 3.4 copy-start.5
  211.5 1.7 copy-start.2
  232.8 165.8 %all-to-all-start.1 = ((bf16[32,1,256,128]{3,2,1,0:T(8,128)(2,1)}), bf16[32,1,256,128]{3,2,1,0:T(8,128)(2,1)}, u32[]{:S(2)}, u32[]{:S(2)}) async-start(bf16[32,1,256,128]{3,2,1,0:T(8,128)(2,1)} %copy.32), calls=%async_computation.1 | async-start | bytes 4194304 | tf_op jit(solution)/shard_map/all_to_all | solution.py:92
  254.9 162.7 %all-reduce.5.cloned.1.call-start = ((), (), s32[]{:S(2)}) async-start(), calls=%async_computation.8 | async-start | bytes 966656 | tf_op jit(solution)/shard_map/psum | solution.py:105
  258.1 124.5 %copy-start.7 = (f32[256,26]{0,1:T(8,128)S(1)}, f32[256,26]{0,1:T(8,128)}, u32[]{:S(2)}) copy-start(f32[256,26]{0,1:T(8,128)} %convert_element_type.79) | copy-start | bytes 79876
  385.6 6.5 %copy-start.9 = (bf16[256,128]{1,0:T(8,128)(2,1)S(1)}, bf16[256,128]{1,0:T(8,128)(2,1)}, u32[]{:S(2)}) copy-start(bf16[256,128]{1,0:T(8,128)(2,1)} %param.11) | copy-start | bytes 196612
Sparse Core Ops, SparseCore 0:
  10.3 49.8 all-gather.4
  62.4 45.7 all-gather.2
  112.2 111.3 reduce-scatter.6
  227.4 121.7 reduce-scatter.4
  392.2 25.4 all-reduce.4
where the time goes:
time: 429 us; the launch traced here: 428 us
  blocking collectives  200 us (47%)
  waiting for transfers between devices  99.7 us (23%)
  local copies, waits for them, and re-layouts  42.9 us (10%)
  matrix products  28.8 us (7%)
  starting transfers between devices  26.8 us (6%)
  between operations  15.3 us (4%)
  other arithmetic  14 us (3%)
    unnamed x2, blocking collectives  195 us
    all_gather x1, waiting for transfers between devices, local(): lax.all_gather(proj_up, 'wide', axis=1, tiled=True)  51.4 us
    all_gather x1, waiting for transfers between devices, local(): lax.all_gather(down_projection, 'wide', axis=0, tiled=True)  30.9 us
    all_to_all x1, starting transfers between devices, local(): lax.all_to_all(slot_grad.reshape(slot_count, 1, samples, feature_index),...  22.1 us
    unnamed x30, local copies, waits for them, and re-layouts  19 us
    psum x1, waiting for transfers between devices, local(): lax.psum(shares[0].astype(jnp.bfloat16), 'pair').astype(jnp.float32)  15.9 us
    dot_general x2, matrix products, cross_forward(): projected = jnp.dot(low_rank, up, preferred_element_type=jnp.float32)  9.97 us
  transfers between devices with their start and end apart: 7, of which 3 were waited for; matrix products, arithmetic and copies ran while one was open for 18% of the time, Pallas kernels for 0%

commit v1 on v0

v1 whole, which is shorter than its diff:
```python
import functools

import jax
import jax.numpy as jnp
from jax import lax
from jax.experimental import pallas as pl
from jax.experimental.pallas import tpu as pltpu
from jax.sharding import PartitionSpec as P

MESH = pl.DeviceIdType.MESH


def flipped(index, mask):
    out = index
    bit = 1
    while bit <= mask:
        if mask & bit:
            out = out + bit - 2 * bit * lax.rem(index // bit, 2)
        bit *= 2
    return out


def stage_list(wide):
    stages = []
    mask = wide // 2
    while mask > 1:
        stages.append(("wide", mask))
        mask //= 2
    return stages + [("pair", 1), ("wide", 1)]


def meet(stages, partner):
    barrier = pltpu.get_barrier_semaphore()
    for stage in stages:
        pl.semaphore_signal(barrier, inc=1, device_id=partner(stage), device_id_type=MESH)
    pl.semaphore_wait(barrier, len(stages))


def gather_kernel(
    wide, down_ref, up_ref, vec_ref, down_out, up_out, vec_out,
    vec_held, vec_got, send_sem, recv_sem, local_sem, vec_send, vec_recv,
):
    me = lax.axis_index("wide")
    pair = lax.axis_index("pair")
    stages = stage_list(wide)
    half = down_ref.shape[1] // 2
    starts = (pl.multiple_of(pair * half, half), pl.multiple_of((1 - pair) * half, half))
    ins, outs = (down_ref, up_ref), (down_out, up_out)

    def partner(stage):
        if stage[0] == "pair":
            return {"pair": 1 - pair}
        return {"wide": flipped(me, stage[1])}

    meet(stages, partner)
    sends = []

    def copy(stage, source, part, kind, received, which):
        columns = pl.ds(starts[part], half)
        block = flipped(me, source)
        if source == 0:
            src = ins[kind].at[:, columns]
        else:
            src = outs[kind].at[block, :, columns]
        return pltpu.make_async_remote_copy(
            src_ref=src,
            dst_ref=outs[kind].at[block, :, columns],
            send_sem=send_sem.at[which],
            recv_sem=recv_sem.at[received],
            device_id=partner(stage),
            device_id_type=MESH,
        )

    def slot(offset, part, kind):
        return (offset * 2 + part) * 2 + kind

    def forward(position, source, part):
        for stage in stages[position:]:
            if stage[0] == "pair":
                if part == 1 or source == 0:
                    continue
                offset, got_part = source, 1
            else:
                offset, got_part = source ^ stage[1], part
            for kind in range(2):
                made = copy(stage, source, part, kind, slot(offset, got_part, kind), len(sends))
                made.start()
                sends.append(made)

    def await_block(offset, part):
        columns = pl.ds(starts[part], half)
        block = flipped(me, offset)
        for kind in range(2):
            view = outs[kind].at[block, :, columns]
            pltpu.make_async_copy(view, view, recv_sem.at[slot(offset, part, kind)]).wait()

    def vector(index, stage):
        return pltpu.make_async_remote_copy(
            src_ref=vec_held.at[index],
            dst_ref=vec_got.at[index],
            send_sem=vec_send.at[index],
            recv_sem=vec_recv.at[index],
            device_id=partner(stage),
            device_id_type=MESH,
        )

    vec_held[0] = vec_ref[...]
    vectors = [vector(index, stage) for index, stage in enumerate(stages)]
    forward(0, 0, 0)
    forward(len(stages) - 1, 0, 1)
    vectors[0].start()
    own = []
    for kind in range(2):
        keep = pltpu.make_async_copy(ins[kind], outs[kind].at[me], local_sem.at[kind])
        keep.start()
        own.append(keep)

    known = [0]
    for position, stage in enumerate(stages):
        if stage[0] == "pair":
            for offset in known[1:]:
                await_block(offset, 1)
                forward(position + 1, offset, 1)
        elif stage[1] > 1:
            arrived = [offset ^ stage[1] for offset in known]
            for offset in arrived:
                await_block(offset, 0)
                forward(position + 1, offset, 0)
            known = known + arrived
        else:
            for offset in known:
                for part in range(2):
                    await_block(offset ^ 1, part)
        vectors[position].wait_recv()
        total = vec_held[position] + vec_got[position]
        if position + 1 < len(stages):
            vec_held[position + 1] = total
            vectors[position + 1].start()
        else:
            vec_out[...] = total
    for keep in own:
        keep.wait()
    for made in sends + vectors:
        made.wait_send()


def gathered(wide, down, up, vec, collective_id=0):
    rows, rank = down.shape
    count = len(stage_list(wide))
    trees = 2 * (wide // 2 - 1 + wide // 2 - 1 + wide)
    vmem = pl.BlockSpec(memory_space=pltpu.VMEM)
    hbm = pl.BlockSpec(memory_space=pl.ANY)
    return pl.pallas_call(
        functools.partial(gather_kernel, wide),
        out_shape=(
            jax.ShapeDtypeStruct((wide, rows, rank), down.dtype),
            jax.ShapeDtypeStruct((wide, rows, rank), up.dtype),
            jax.ShapeDtypeStruct(vec.shape, vec.dtype),
        ),
        in_specs=[vmem, vmem, vmem],
        out_specs=(hbm, hbm, vmem),
        scratch_shapes=[
            pltpu.VMEM((count,) + vec.shape, vec.dtype),
            pltpu.VMEM((count,) + vec.shape, vec.dtype),
            pltpu.SemaphoreType.DMA((trees,)),
            pltpu.SemaphoreType.DMA((4 * wide,)),
            pltpu.SemaphoreType.DMA((2,)),
            pltpu.SemaphoreType.DMA((count,)),
            pltpu.SemaphoreType.DMA((count,)),
        ],
        compiler_params=pltpu.CompilerParams(
            collective_id=collective_id, has_side_effects=True
        ),
        cost_estimate=pl.CostEstimate(
            flops=0, bytes_accessed=wide * rows * rank * 40, transcendentals=0
        ),
        name="weights_gather",
    )(down, up, vec)


def tree_slots(wide):
    slots = {}
    mask = 2
    while mask < wide:
        for offset in range(0, wide, 2 * mask):
            slots[(mask, offset)] = len(slots)
        mask *= 2
    return slots


def scatter_kernel(
    wide, down_ref, up_ref, down_out, up_out,
    core_got, pair_send, pair_got, tree_send, tree_got, last_send, last_got,
    core_sems, pair_sems, tree_sems, last_sems,
):
    me = lax.axis_index("wide")
    pair = lax.axis_index("pair")
    stages = stage_list(wide)
    slots = tree_slots(wide)
    half = down_ref.shape[2] // 2
    mine = pl.ds(pl.multiple_of(pair * half, half), half)
    other = pl.ds(pl.multiple_of((1 - pair) * half, half), half)
    ins, outs = (down_ref, up_ref), (down_out, up_out)
    evens = list(range(0, wide, 2))
    bits = wide.bit_length()
    order = sorted(
        evens, key=lambda e: [(e >> b) & 1 for b in range(1, bits)], reverse=True
    )

    def partner(stage):
        if stage[0] == "pair":
            return {"pair": 1 - pair}
        return {"wide": flipped(me, stage[1])}

    meet(stages, partner)

    def remote(src, dst, sems, index, stage):
        return pltpu.make_async_remote_copy(
            src_ref=src,
            dst_ref=dst,
            send_sem=sems.at[0, index],
            recv_sem=sems.at[1, index],
            device_id=partner(stage),
            device_id_type=MESH,
        )

    core_copies = {}
    for part, columns in ((1, other), (0, mine)):
        for offset in order:
            for kind in range(2):
                made = remote(
                    ins[kind].at[flipped(me, offset ^ 1), :, columns],
                    core_got.at[kind, offset // 2, :, columns],
                    core_sems,
                    (offset // 2 * 2 + part) * 2 + kind,
                    ("wide", 1),
                )
                made.start()
                core_copies[(part, offset, kind)] = made

    def both_cores(kind, offset, columns):
        own = ins[kind][flipped(me, offset), :, columns].astype(jnp.float32)
        return own + core_got[kind, offset // 2, :, columns].astype(jnp.float32)

    pair_copies = {}
    for offset in order:
        for kind in range(2):
            core_copies[(1, offset, kind)].wait_recv()
            pair_send[kind, offset // 2] = both_cores(kind, offset, other).astype(jnp.bfloat16)
            made = remote(
                pair_send.at[kind, offset // 2],
                pair_got.at[kind, offset // 2],
                pair_sems,
                offset // 2 * 2 + kind,
                ("pair", 1),
            )
            made.start()
            pair_copies[(offset, kind)] = made

    tree_copies = []
    last_copies = []
    for offset in order:
        for kind in range(2):
            core_copies[(0, offset, kind)].wait_recv()
            pair_copies[(offset, kind)].wait_recv()
            total = both_cores(kind, offset, mine)
            total = total + pair_got[kind, offset // 2].astype(jnp.float32)
            mask = 2
            while mask < wide and not offset & mask:
                index = slots[(mask, offset)]
                view = tree_got.at[kind, index]
                pltpu.make_async_copy(view, view, tree_sems.at[1, index * 2 + kind]).wait()
                total = total + tree_got[kind, index].astype(jnp.float32)
                mask *= 2
            if mask < wide:
                index = slots[(mask, offset ^ mask)]
                tree_send[kind, index] = total.astype(jnp.bfloat16)
                made = remote(
                    tree_send.at[kind, index],
                    tree_got.at[kind, index],
                    tree_sems,
                    index * 2 + kind,
                    ("wide", mask),
                )
                made.start()
                tree_copies.append(made)
            else:
                rounded = total.astype(jnp.bfloat16)
                last_send[kind] = rounded
                made = remote(
                    last_send.at[kind], last_got.at[kind], last_sems, kind, ("pair", 1)
                )
                made.start()
                last_copies.append(made)
                outs[kind][:, mine] = rounded.astype(jnp.float32)
    for kind in range(2):
        last_copies[kind].wait_recv()
        outs[kind][:, other] = last_got[kind].astype(jnp.float32)
    for made in list(core_copies.values()) + list(pair_copies.values()):
        made.wait_send()
    for made in tree_copies + last_copies:
        made.wait_send()


def scattered(wide, grad_down, grad_up, collective_id=1):
    _, rows, rank = grad_down.shape
    half = rank // 2
    slots = len(tree_slots(wide))
    vmem = pl.BlockSpec(memory_space=pltpu.VMEM)
    held = jnp.bfloat16
    return pl.pallas_call(
        functools.partial(scatter_kernel, wide),
        out_shape=(
            jax.ShapeDtypeStruct((rows, rank), jnp.float32),
            jax.ShapeDtypeStruct((rows, rank), jnp.float32),
        ),
        in_specs=[vmem, vmem],
        out_specs=(vmem, vmem),
        scratch_shapes=[
            pltpu.VMEM((2, wide // 2, rows, rank), held),
            pltpu.VMEM((2, wide // 2, rows, half), held),
            pltpu.VMEM((2, wide // 2, rows, half), held),
            pltpu.VMEM((2, slots, rows, half), held),
            pltpu.VMEM((2, slots, rows, half), held),
            pltpu.VMEM((2, rows, half), held),
            pltpu.VMEM((2, rows, half), held),
            pltpu.SemaphoreType.DMA((2, 2 * wide)),
            pltpu.SemaphoreType.DMA((2, wide)),
            pltpu.SemaphoreType.DMA((2, 2 * slots)),
            pltpu.SemaphoreType.DMA((2, 2)),
        ],
        compiler_params=pltpu.CompilerParams(
            collective_id=collective_id, has_side_effects=True,
            vmem_limit_bytes=40 * 1024 * 1024,
        ),
        cost_estimate=pl.CostEstimate(
            flops=0, bytes_accessed=wide * rows * rank * 40, transcendentals=0
        ),
        name="gradients_scatter",
    )(grad_down, grad_up)


def table_means(slot_rows, lookup_count, table_slots):
    picked = jnp.take(slot_rows, table_slots, axis=0).astype(jnp.float32)
    scaled = picked / jnp.transpose(lookup_count).astype(jnp.float32)[:, :, None]
    return jnp.transpose(scaled, (1, 0, 2)).reshape(scaled.shape[1], -1).astype(jnp.bfloat16)


OVER_ROWS = (((0,), (0,)), ((), ()))
OVER_COLS = (((1,), (1,)), ((), ()))


def dot(left, right, dims):
    return lax.dot_general(left, right, dims, preferred_element_type=jnp.float32)


def cross_forward(stacked, down, up_rows):
    low_rank = jnp.dot(stacked, down, preferred_element_type=jnp.float32).astype(jnp.bfloat16)
    return low_rank, dot(low_rank, up_rows, OVER_COLS)


def local(
    wide,
    pooled_b,
    dense_output_second,
    counts_b,
    slot_of,
    stacked_a,
    upstream_a,
    counts_a,
    down_projection,
    proj_up,
    cross_layer_bias,
):
    feature = dense_output_second.shape[1]
    tables = counts_b.shape[1]
    table_slots = slot_of[:tables]
    shard = down_projection.shape[0]
    rank = down_projection.shape[1]
    width = stacked_a.shape[1]
    samples = stacked_a.shape[0]
    me = lax.axis_index("wide")
    lanes = -(-shard // 128) * 128

    stacked_wide = stacked_a.astype(jnp.float32)
    upstream_wide = upstream_a.astype(jnp.float32)
    scale_grad = upstream_wide * stacked_wide
    bias_share = jnp.sum(scale_grad, axis=0).reshape(wide, shard)
    holds = (jnp.arange(wide) == me) & (lax.axis_index("pair") == 0)
    bias_own = jnp.where(holds[:, None], cross_layer_bias.astype(jnp.float32)[None, :], 0.0)
    vec = jnp.pad(jnp.concatenate([bias_share, bias_own], axis=0), ((0, 0), (0, lanes - shard)))
    down_all, up_all, vec_all = gathered(wide, down_projection, jnp.transpose(proj_up), vec)
    grad_bias = lax.dynamic_index_in_dim(vec_all, me, 0, keepdims=False)[:shard]
    bias = vec_all[wide:, :shard].reshape(width)

    pooled_b, down_all = lax.optimization_barrier((pooled_b, down_all))
    arrived = lax.all_to_all(pooled_b, "wide", split_axis=1, concat_axis=0, tiled=True)
    slot_count = arrived.shape[0]

    down = down_all.reshape(width, rank)
    up_rows = up_all.reshape(width, rank)

    proj_grad = scale_grad.astype(jnp.bfloat16)
    low_grad = jnp.dot(proj_grad, up_rows, preferred_element_type=jnp.float32).astype(jnp.bfloat16)
    low_a, projected = cross_forward(stacked_a, down, up_rows)
    input_grad = upstream_wide * (projected + bias) + upstream_wide
    input_grad = input_grad + dot(low_grad, down, OVER_COLS)
    grad_down = dot(stacked_a, low_grad, OVER_ROWS).astype(jnp.bfloat16)
    grad_up = dot(proj_grad, low_a, OVER_ROWS).astype(jnp.bfloat16)
    dense_gradient = input_grad[:, :feature].astype(jnp.bfloat16)
    table_gradient = (
        input_grad[:, feature:].reshape(samples, -1, feature)
        / counts_a.astype(jnp.float32)[:, :, None]
    )
    table_gradient = jnp.transpose(table_gradient, (1, 0, 2)).astype(jnp.bfloat16)
    slot_selector = (
        table_slots[None, :] == jnp.arange(slot_count, dtype=jnp.int32)[:, None]
    ).astype(jnp.bfloat16)
    slot_grad = jnp.einsum(
        "qv,vxk->qxk", slot_selector, table_gradient, preferred_element_type=jnp.float32
    ).astype(jnp.bfloat16)
    slot_grad, grad_down, grad_up = lax.optimization_barrier((slot_grad, grad_down, grad_up))
    returned = lax.all_to_all(
        slot_grad.reshape(slot_count, 1, samples, feature),
        "wide",
        split_axis=0,
        concat_axis=1,
        tiled=True,
    )
    down_sum, up_sum = scattered(
        wide, grad_down.reshape(wide, shard, rank), grad_up.reshape(wide, shard, rank)
    )

    slot_rows = arrived.reshape(slot_count, samples, feature)
    stacked_b = jnp.concatenate(
        [dense_output_second, table_means(slot_rows, counts_b, table_slots)], axis=1
    )
    _, projected_b = cross_forward(stacked_b, down, up_rows)
    b_wide = stacked_b.astype(jnp.float32)
    crossed_b = (b_wide * (projected_b + bias) + b_wide).astype(jnp.bfloat16)
    return (crossed_b, dense_gradient, returned, down_sum, jnp.transpose(up_sum), grad_bias)


def solution(mesh):
    return jax.shard_map(
        functools.partial(local, mesh.shape["wide"]),
        mesh=mesh,
        in_specs=(
            P("wide", None, "pair", None),
            P(("wide", "pair"), None),
            P(("wide", "pair"), None),
            P(),
            P(("wide", "pair"), None),
            P(("wide", "pair"), None),
            P(("wide", "pair"), None),
            P("wide", None),
            P(None, "wide"),
            P("wide"),
        ),
        out_specs=(
            P(("wide", "pair"), None),
            P(("wide", "pair"), None),
            P("wide", None, "pair", None),
            P("wide", None),
            P(None, "wide"),
            P("wide"),
        ),
        check_vma=False,
    )
```

time: 429 us -> 209 us (0.49)
  blocking collectives: 200 us -> 0 us
  Pallas kernels: 0 us -> 110 us
  waiting for transfers between devices: 99.7 us -> 6.48 us
  between operations: 15.3 us -> 0.95 us
  starting transfers between devices: 26.8 us -> 17.2 us
  matrix products: 28.8 us -> 19.8 us
    unnamed x2 -> x0, blocking collectives: 195 us -> none
    pallas_call x0 -> x2, Pallas kernels: none -> 110 us  [the longest x1 55.4 us: gathered(): pl.pallas_call(functools.partial(gather_kernel, wide), out_shape=(jax.Sha...]
    all_gather x2 -> x0, waiting for transfers between devices: 82.4 us -> none  [the longest x1 51.4 us: local(): lax.all_gather(proj_up, 'wide', axis=1, tiled=True)]
    psum x1 -> x0, waiting for transfers between devices: 15.9 us -> none  [local(): lax.psum(shares[0].astype(jnp.bfloat16), 'pair').astype(jnp.float32)]
    unnamed x30 -> x42, local copies, waits for them, and re-layouts: 19 us -> 7.78 us
    all_to_all x1, starting transfers between devices: 22.1 us -> 11.3 us  [local(): lax.all_to_all(slot_grad.reshape(slot_count, 1, samples, feature), 'wide'...]
    dot_general x6, matrix products: 23.4 us -> 14.1 us  [the longest x5 13 us: dot(): lax.dot_general(left, right, dims, preferred_element_type=jnp.float32)]
    optimization_barrier x0 -> x2, local copies, waits for them, and re-layouts: none -> 9.02 us  [the longest x1 5.76 us: local(): lax.optimization_barrier((slot_grad, grad_down, grad_up))]
  transfers between devices with their start and end apart: 7 -> 2, of which waited for: 3 -> 1; matrix products, arithmetic and copies ran while one was open for 18% -> 24% of each run, Pallas kernels for 0% -> 26%
where the time goes in v1:
time: 209 us; the launch traced here: 208 us
  Pallas kernels  110 us (53%)
  local copies, waits for them, and re-layouts  43 us (21%)
  matrix products  19.8 us (9%)
  starting transfers between devices  17.2 us (8%)
  other arithmetic  10.9 us (5%)
  waiting for transfers between devices  6.48 us (3%)
    pallas_call x1, Pallas kernels, gathered(): pl.pallas_call(functools.partial(gather_kernel, wide), out_shape=(jax.Sha...  55.4 us
    pallas_call x1, Pallas kernels, scattered(): pl.pallas_call(functools.partial(scatter_kernel, wide), out_shape=(jax.Sh...  54.4 us
    dot_general x5, matrix products, dot(): lax.dot_general(left, right, dims, preferred_element_type=jnp.float32)  13 us
    all_to_all x1, starting transfers between devices, local(): lax.all_to_all(slot_grad.reshape(slot_count, 1, samples, feature), 'wide'...  11.3 us
    unnamed x42, local copies, waits for them, and re-layouts  7.78 us
    slice x2, local copies, waits for them, and re-layouts, local(): input_grad[:, feature:].reshape(samples, -1, feature)  6.98 us
    all_to_all x1, waiting for transfers between devices, local(): lax.all_to_all(pooled_b, 'wide', split_axis=1, concat_axis=0, tiled=True)  6.47 us
    all_to_all x1, starting transfers between devices, local(): lax.all_to_all(pooled_b, 'wide', split_axis=1, concat_axis=0, tiled=True)  5.97 us
  transfers between devices with their start and end apart: 2, of which 1 were waited for; matrix products, arithmetic and copies ran while one was open for 24% of the time, Pallas kernels for 26%

profile of v1, /device:TPU:0, one launch (start us, length us, event | category | flops | bytes accessed | tf_op | source)
XLA Modules:
  0.0 208.1 jit_solution(8543836446981028690)
XLA Ops:
  0.6 0.7 convert_element_type.72
  1.3 2.5 %fusion.8 = f32[3456]{0:T(1024)S(1)} fusion(bf16[256,3456]{1,0:T(8,128)(2,1)} %param.14, bf16[256,3456]{1,0:T(8,128)(2,1)} %param.15), kind=kLoop, calls=%fused_computation.17 | loop fusion | flops 3535488 | bytes 3552768 | tf_op jit(solution)/shard_map/reduce_sum | solution.py:388
  3.8 0.1 reshape.55
  3.9 0.1 broadcast_select_fusion
  4.0 0.6 select_maximum_fusion.vec_ref
  4.6 55.4 %weights_gather.1 = (bf16[16,216,512]{2,1,0:T(8,128)(2,1)}, bf16[16,216,512]{2,1,0:T(8,128)(2,1)}, f32[32,256]{1,0:T(8,128)}) custom-call(bf16[216,512]{1,0:T(8,128)(2,1)} %down_ref.1, bf16[216,512]{1,0:T(8,128)(2,1)} %bitcast.59, f32[32,256]{1,0:T(8,128)} %select_maximum_fusion.vec_ref), custom_call_target="tpu_custom_call" | custom-call | bytes 70778880 | tf_op jit(solution)/shard_map/weights_gather/pallas_call | solution.py:153
  60.0 0.0 copy-start.5
  60.0 3.3 %copy.27 = bf16[2,16,256,128]{3,2,0,1:T(8,128)(2,1)} copy(bf16[2,16,256,128]{3,2,1,0:T(8,128)(2,1)} %param.10) | data formatting | bytes 4194304 | tf_op jit(solution)/shard_map/optimization_barrier | solution.py:396
  63.3 6.0 %all-to-all-start = ((bf16[2,16,256,128]{3,2,0,1:T(8,128)(2,1)}), bf16[2,16,256,128]{3,2,0,1:T(8,128)(2,1)}, u32[]{:S(2)}, u32[]{:S(2)}) async-start(bf16[2,16,256,128]{3,2,0,1:T(8,128)(2,1)} %copy.27), calls=%async_computation | async-start | bytes 4194304 | tf_op jit(solution)/shard_map/all_to_all | solution.py:397
  69.2 0.0 copy-start.7
  69.3 1.5 convert_element_type.84
  70.8 1.3 slice.20
  72.1 0.8 add.36
  72.9 0.0 copy-start.10
  72.9 0.0 copy-done.5
  72.9 3.3 %convolution_convert_fusion.4 = bf16[512,256]{1,0:T(8,128)(2,1)S(1)} fusion(bf16[3456,512]{1,0:T(8,128)(2,1)} %bitcast.55, bf16[256,3456]{1,0:T(8,128)(2,1)S(1)} %copy-done.5), kind=kOutput, calls=%fused_computation.23 | convolution fusion | flops 906100736 | bytes 5570560 | tf_op jit(solution)/shard_map/dot_general | solution.py:358
  76.2 0.0 copy-start.12
  76.3 0.0 copy-done.7
  76.3 0.0 copy-done.10
  76.3 1.2 fusion.1
  77.5 0.0 copy-done.12
  77.5 0.0 copy-start.11
  77.5 1.1 convolution_convert_fusion.3
  78.6 0.9 copy-done.11
  79.5 1.1 convolution_add_fusion
  80.6 0.0 copy-done.14
  80.7 0.0 copy-start.9
  80.7 1.8 copy-done.9
  82.5 1.9 slice.28
  84.4 5.0 %copy.30 = f32[256,3328]{0,1:T(8,128)} copy(f32[256,3328]{1,0:T(8,128)} %slice.28) | data formatting | bytes 6815744 | tf_op jit(solution)/shard_map/slice | solution.py:412
  89.4 0.0 copy-done.17
  89.4 2.4 %fusion.9 = bf16[26,256,128]{1,2,0:T(8,128)(2,1)S(1)} fusion(f32[256,26,128]{0,2,1:T(8,128)} %bitcast.49, f32[256,26]{0,1:T(8,128)S(1)} %copy-done.17), kind=kLoop, calls=%fused_computation.21 | loop fusion | flops 1703936 | bytes 5138432 | tf_op jit(solution)/shard_map/convert_element_type | solution.py:415
  91.8 3.4 %copy.31 = bf16[26,256,128]{2,0,1:T(8,128)(2,1)} copy(bf16[26,256,128]{1,2,0:T(8,128)(2,1)S(1)} %fusion.9) | data formatting | bytes 3407872 | tf_op jit(solution)/shard_map/convert_element_type | solution.py:415
  95.3 2.3 %convolution_convert_fusion.2 = bf16[32,256,128]{2,0,1:T(8,128)(2,1)S(1)} fusion(bf16[26,256,128]{2,0,1:T(8,128)(2,1)} %copy.31, s32[26]{0:T(128)S(1)} %bitcast.61), kind=kOutput, calls=%fused_computation.19 | convolution fusion | flops 55575360 | bytes 3801192 | tf_op jit(solution)/shard_map/qv,vxk->qxk/dot_general | solution.py:419
  97.6 0.0 copy-start.6
  97.6 0.0 copy-start.8
  97.6 0.0 copy-start.13
  97.6 2.9 %fusion.4 = bf16[3456,512]{0,1:T(8,128)(2,1)} fusion(bf16[256,512]{1,0:T(8,128)(2,1)S(1)} %copy-done.15, bf16[256,3456]{1,0:T(8,128)(2,1)S(1)} %copy-done.5), kind=kOutput, calls=%fused_computation.10 | convolution fusion | flops 907739136 | bytes 5570560 | tf_op jit(solution)/shard_map/dot_general | solution.py:354
  100.5 0.0 copy-done.6
  100.5 0.0 copy-done.13
  100.5 1.1 convolution_convert_fusion
  101.7 2.1 %copy.32 = bf16[32,1,256,128]{3,2,1,0:T(8,128)(2,1)} copy(bf16[32,1,256,128]{3,0,2,1:T(8,128)(2,1)S(1)} %bitcast.50) | data formatting | bytes 4194304 | tf_op jit(solution)/shard_map/reshape | solution.py:424
  103.8 6.5 %all-to-all-done = bf16[2,16,256,128]{3,2,0,1:T(8,128)(2,1)} async-done(((bf16[2,16,256,128]{3,2,0,1:T(8,128)(2,1)}), bf16[2,16,256,128]{3,2,0,1:T(8,128)(2,1)}, u32[]{:S(2)}, u32[]{:S(2)}) %all-to-all-start) | async-done | bytes 2097184 | tf_op jit(solution)/shard_map/all_to_all | solution.py:397
  110.3 11.3 %all-to-all-start.1 = ((bf16[32,1,256,128]{3,2,1,0:T(8,128)(2,1)}), bf16[32,1,256,128]{3,2,1,0:T(8,128)(2,1)}, u32[]{:S(2)}, u32[]{:S(2)}) async-start(bf16[32,1,256,128]{3,2,1,0:T(8,128)(2,1)} %copy.32), calls=%async_computation.1 | async-start | bytes 4194304 | tf_op jit(solution)/shard_map/all_to_all | solution.py:423
  121.6 1.5 slice.31
  123.1 1.4 convert_element_type.75
  124.5 5.8 %copy.34 = bf16[3456,512]{1,0:T(8,128)(2,1)} copy(bf16[3456,512]{0,1:T(8,128)(2,1)} %fusion.4) | data formatting | bytes 7077888 | tf_op jit(solution)/shard_map/optimization_barrier | solution.py:422
  130.2 2.0 copy-done
  132.2 54.4 %gradients_scatter.1 = (f32[216,512]{1,0:T(8,128)S(1)}, f32[216,512]{1,0:T(8,128)S(1)}) custom-call(bf16[16,216,512]{2,1,0:T(8,128)(2,1)S(1)} %bitcast.47, bf16[16,216,512]{2,1,0:T(8,128)(2,1)S(1)} %bitcast.46), custom_call_target="tpu_custom_call" | custom-call | bytes 70778880 | tf_op jit(solution)/shard_map/gradients_scatter/pallas_call | solution.py:311
  186.6 0.0 copy-start.1
  186.6 0.7 copy-done.1
  187.4 0.8 copy-done.3
  188.2 1.3 constant_dynamic-slice_fusion
  189.4 0.7 compare_and_fusion.1
  190.1 2.5 %gather_fusion = bf16[26,256,128]{2,1,0:T(8,128)(2,1)S(1)} fusion(bf16[32,256,128]{2,1,0:T(8,128)(2,1)} %bitcast.3, s32[1024]{0:T(1024)S(1)} %pad_clamp_fusion), kind=kCustom, calls=%fused_computation | custom fusion | bytes 3407976 | tf_op jit(solution)/shard_map/jit(_take)/gather | solution.py:344
  192.6 1.2 fusion.6
  193.7 1.8 copy.28
  195.5 0.0 copy-start.19
  195.5 1.3 copy.29
  196.8 0.0 all-to-all-done.1
  196.8 3.1 %copy.36 = bf16[16,2,1,256,128]{4,3,0,1,2:T(8,128)(2,1)} copy(bf16[16,2,1,256,128]{4,3,1,0,2:T(8,128)(2,1)} %bitcast.13) | data formatting | bytes 4194304 | tf_op jit(solution)/shard_map/all_to_all | solution.py:423
  200.0 6.6 %fusion.5 = bf16[256,3456]{1,0:T(8,128)(2,1)} fusion(bf16[3456,512]{1,0:T(8,128)(2,1)} %bitcast.52, f32[3456]{0:T(1024)S(1)} %add.36, bf16[256,3328]{1,0:T(8,128)(2,1)S(1)} %copy.29, bf16[256,128]{1,0:T(8,128)(2,1)S(1)} %copy-done.19, bf16[3456,512]{1,0:T(8,128)(2,1)} %bitcast.56), kind=kOutput, calls=%fused_computation.11 | convolution fusion | flops 1822687232 | bytes 10630656 | tf_op jit(solution)/shard_map/dot_general | solution.py:354
  206.6 0.8 copy.39
  207.4 0.8 copy.40
  (18 shorter events, 0.0 us)
Async XLA Ops:
  60.0 12.9 %copy-start.5 = (bf16[256,3456]{1,0:T(8,128)(2,1)S(1)}, bf16[256,3456]{1,0:T(8,128)(2,1)}, u32[]{:S(2)}) copy-start(bf16[256,3456]{1,0:T(8,128)(2,1)} %param.14) | copy-start | bytes 5308420
  63.3 47.0 %all-to-all-start = ((bf16[2,16,256,128]{3,2,0,1:T(8,128)(2,1)}), bf16[2,16,256,128]{3,2,0,1:T(8,128)(2,1)}, u32[]{:S(2)}, u32[]{:S(2)}) async-start(bf16[2,16,256,128]{3,2,0,1:T(8,128)(2,1)} %copy.27), calls=%async_computation | async-start | bytes 4194304 | tf_op jit(solution)/shard_map/all_to_all | solution.py:397
  69.2 7.0 %copy-start.7 = (bf16[256,3456]{1,0:T(8,128)(2,1)S(1)}, bf16[256,3456]{1,0:T(8,128)(2,1)}, u32[]{:S(2)}) copy-start(bf16[256,3456]{1,0:T(8,128)(2,1)} %param.15) | copy-start | bytes 5308420
  72.9 3.4 %copy-start.10 = (bf16[16,216,512]{2,1,0:T(8,128)(2,1)S(1)}, bf16[16,216,512]{2,1,0:T(8,128)(2,1)}, u32[]{:S(2)}) copy-start(bf16[16,216,512]{2,1,0:T(8,128)(2,1)} %get-tuple-element.19) | copy-start | bytes 10616836
  76.2 1.2 copy-start.12
  77.5 2.0 copy-start.11
  79.5 1.2 copy-start.14
  80.7 1.8 copy-start.9
  84.4 5.1 %copy-start.17 = (f32[256,26]{0,1:T(8,128)S(1)}, f32[256,26]{0,1:T(8,128)}, u32[]{:S(2)}) copy-start(f32[256,26]{0,1:T(8,128)} %convert_element_type.84) | copy-start | bytes 79876
  89.4 5.8 %copy-start.18 = (s32[32]{0:T(128)S(1)}, s32[32]{0:T(128)}, u32[]{:S(2)}) copy-start(s32[32]{0:T(128)} %param.13) | copy-start | bytes 388
  95.2 2.3 %copy-start.15 = (bf16[256,512]{1,0:T(8,128)(2,1)S(1)}, bf16[256,512]{1,0:T(8,128)(2,1)}, u32[]{:S(2)}) copy-start(bf16[256,512]{1,0:T(8,128)(2,1)} %copy-done.14) | copy-start | bytes 786436
  97.6 3.0 %copy-start.6 = (bf16[256,3456]{1,0:T(8,128)(2,1)S(1)}, bf16[256,3456]{1,0:T(8,128)(2,1)}, u32[]{:S(2)}) copy-start(bf16[256,3456]{1,0:T(8,128)(2,1)} %param.14) | copy-start | bytes 5308420
  97.6 2.9 %copy-start.8 = (bf16[256,3456]{1,0:T(8,128)(2,1)S(1)}, bf16[256,3456]{1,0:T(8,128)(2,1)}, u32[]{:S(2)}) copy-start(bf16[256,3456]{1,0:T(8,128)(2,1)} %param.15) | copy-start | bytes 5308420
  97.6 2.9 %copy-start.13 = (bf16[512,256]{1,0:T(8,128)(2,1)S(1)}, bf16[512,256]{1,0:T(8,128)(2,1)}, u32[]{:S(2)}) copy-start(bf16[512,256]{1,0:T(8,128)(2,1)} %copy-done.12) | copy-start | bytes 786436
  110.3 86.5 %all-to-all-start.1 = ((bf16[32,1,256,128]{3,2,1,0:T(8,128)(2,1)}), bf16[32,1,256,128]{3,2,1,0:T(8,128)(2,1)}, u32[]{:S(2)}, u32[]{:S(2)}) async-start(bf16[32,1,256,128]{3,2,1,0:T(8,128)(2,1)} %copy.32), calls=%async_computation.1 | async-start | bytes 4194304 | tf_op jit(solution)/shard_map/all_to_all | solution.py:423
  130.2 2.0 copy-start
  186.6 0.8 copy-start.1
  187.4 0.8 copy-start.3
  188.1 4.4 %copy-start.16 = (f32[256,26]{0,1:T(8,128)S(1)}, f32[256,26]{0,1:T(8,128)}, u32[]{:S(2)}) copy-start(f32[256,26]{0,1:T(8,128)} %convert_element_type.75) | copy-start | bytes 79876
  195.5 4.5 %copy-start.19 = (bf16[256,128]{1,0:T(8,128)(2,1)S(1)}, bf16[256,128]{1,0:T(8,128)(2,1)}, u32[]{:S(2)}) copy-start(bf16[256,128]{1,0:T(8,128)(2,1)} %param.11) | copy-start | bytes 196612
  200.0 6.6 %copy-start.4 = (f32[216,512]{1,0:T(8,128)S(1)}, f32[216,512]{1,0:T(8,128)}, u32[]{:S(2)}) copy-start(f32[216,512]{1,0:T(8,128)} %copy-done.3) | copy-start | bytes 1327108
  200.0 7.4 %copy-start.2 = (f32[216,512]{1,0:T(8,128)S(1)}, f32[216,512]{1,0:T(8,128)}, u32[]{:S(2)}) copy-start(f32[216,512]{1,0:T(8,128)} %copy-done.1) | copy-start | bytes 1327108

commit v2 on v1

--- a/solution.py
+++ b/solution.py
@@ -29,16 +29,38 @@
     return stages + [("pair", 1), ("wide", 1)]
 
 
-def meet(stages, partner):
+def meet(wide, me, pair):
     barrier = pltpu.get_barrier_semaphore()
-    for stage in stages:
-        pl.semaphore_signal(barrier, inc=1, device_id=partner(stage), device_id_type=MESH)
-    pl.semaphore_wait(barrier, len(stages))
+    for offset in range(1, wide):
+        pl.semaphore_signal(
+            barrier, inc=1, device_id={"wide": flipped(me, offset)}, device_id_type=MESH
+        )
+    pl.semaphore_signal(barrier, inc=1, device_id={"pair": 1 - pair}, device_id_type=MESH)
+    pl.semaphore_wait(barrier, wide)
+
+
+def exchange(wide, me, source, target, sems):
+    copies = []
+    for offset in range(wide - 1, 0, -1):
+        peer = flipped(me, offset)
+        made = pltpu.make_async_remote_copy(
+            src_ref=source(peer),
+            dst_ref=target(me),
+            send_sem=sems.at[0, offset],
+            recv_sem=sems.at[1, offset],
+            device_id={"wide": peer},
+            device_id_type=MESH,
+        )
+        made.start()
+        copies.append(made)
+    keep = pltpu.make_async_copy(source(me), target(me), sems.at[0, 0])
+    keep.start()
+    return copies, keep
 
 
 def gather_kernel(
-    wide, down_ref, up_ref, vec_ref, down_out, up_out, vec_out,
-    vec_held, vec_got, send_sem, recv_sem, local_sem, vec_send, vec_recv,
+    wide, down_ref, up_ref, vec_ref, pooled_ref, down_out, up_out, vec_out, arrived_out,
+    vec_held, vec_got, send_sem, recv_sem, local_sem, vec_send, vec_recv, swap_sems,
 ):
     me = lax.axis_index("wide")
     pair = lax.axis_index("pair")
@@ -52,7 +74,7 @@
             return {"pair": 1 - pair}
         return {"wide": flipped(me, stage[1])}
 
-    meet(stages, partner)
+    meet(wide, me, pair)
     sends = []
 
     def copy(stage, source, part, kind, received, which):
@@ -115,8 +137,18 @@
         keep.start()
         own.append(keep)
 
+    each = pooled_ref.shape[0]
+    swaps = None
     known = [0]
     for position, stage in enumerate(stages):
+        if swaps is None and (stage[0] == "pair" or stage[1] == 2):
+            swaps, stay = exchange(
+                wide,
+                me,
+                lambda peer: pooled_ref.at[:, peer],
+                lambda owner: arrived_out.at[pl.ds(owner * each, each)],
+                swap_sems,
+            )
         if stage[0] == "pair":
             for offset in known[1:]:
                 await_block(offset, 1)
@@ -138,13 +170,15 @@
             vectors[position + 1].start()
         else:
             vec_out[...] = total
-    for keep in own:
+    for keep in own + [stay]:
         keep.wait()
+    for made in swaps:
+        made.wait()
     for made in sends + vectors:
         made.wait_send()
 
 
-def gathered(wide, down, up, vec, collective_id=0):
+def gathered(wide, down, up, vec, pooled, collective_id=0):
     rows, rank = down.shape
     count = len(stage_list(wide))
     trees = 2 * (wide // 2 - 1 + wide // 2 - 1 + wide)
@@ -156,9 +190,10 @@
             jax.ShapeDtypeStruct((wide, rows, rank), down.dtype),
             jax.ShapeDtypeStruct((wide, rows, rank), up.dtype),
             jax.ShapeDtypeStruct(vec.shape, vec.dtype),
-        ),
-        in_specs=[vmem, vmem, vmem],
-        out_specs=(hbm, hbm, vmem),
+            jax.ShapeDtypeStruct((pooled.shape[0] * wide,) + pooled.shape[2:], pooled.dtype),
+        ),
+        in_specs=[vmem, vmem, vmem, hbm],
+        out_specs=(hbm, hbm, vmem, hbm),
         scratch_shapes=[
             pltpu.VMEM((count,) + vec.shape, vec.dtype),
             pltpu.VMEM((count,) + vec.shape, vec.dtype),
@@ -167,6 +202,7 @@
             pltpu.SemaphoreType.DMA((2,)),
             pltpu.SemaphoreType.DMA((count,)),
             pltpu.SemaphoreType.DMA((count,)),
+            pltpu.SemaphoreType.DMA((2, wide)),
         ],
         compiler_params=pltpu.CompilerParams(
             collective_id=collective_id, has_side_effects=True
@@ -175,7 +211,7 @@
             flops=0, bytes_accessed=wide * rows * rank * 40, transcendentals=0
         ),
         name="weights_gather",
-    )(down, up, vec)
+    )(down, up, vec, pooled)
 
 
 def tree_slots(wide):
@@ -189,9 +225,11 @@
 
 
 def scatter_kernel(
-    wide, down_ref, up_ref, down_out, up_out,
-    core_got, pair_send, pair_got, tree_send, tree_got, last_send, last_got,
-    core_sems, pair_sems, tree_sems, last_sems,
+    wide, down_ref, up_ref, slot_grad_ref, slot_ref, arrived_ref, dense_ref, counts_ref,
+    weight_down_ref, weight_up_ref, bias_ref,
+    down_out, up_out, returned_out, crossed_out,
+    stacked_held, low_held, core_got, pair_send, pair_got, tree_send, tree_got, last_send, last_got,
+    core_sems, pair_sems, tree_sems, last_sems, swap_sems,
 ):
     me = lax.axis_index("wide")
     pair = lax.axis_index("pair")
@@ -212,7 +250,7 @@
             return {"pair": 1 - pair}
         return {"wide": flipped(me, stage[1])}
 
-    meet(stages, partner)
+    meet(wide, me, pair)
 
     def remote(src, dst, sems, index, stage):
         return pltpu.make_async_remote_copy(
@@ -237,6 +275,15 @@
                 )
                 made.start()
                 core_copies[(part, offset, kind)] = made
+
+    each = returned_out.shape[0]
+    swaps, stay = exchange(
+        wide,
+        me,
+        lambda peer: slot_grad_ref.at[pl.ds(peer * each, each)],
+        lambda owner: returned_out.at[:, owner],
+        swap_sems,
+    )
 
     def both_cores(kind, offset, columns):
         own = ins[kind][flipped(me, offset), :, columns].astype(jnp.float32)
@@ -256,6 +303,11 @@
             )
             made.start()
             pair_copies[(offset, kind)] = made
+
+    forward_b(
+        slot_ref, arrived_ref, dense_ref, counts_ref, weight_down_ref, weight_up_ref, bias_ref,
+        crossed_out, stacked_held, low_held,
+    )
 
     tree_copies = []
     last_copies = []
@@ -300,23 +352,32 @@
         made.wait_send()
     for made in tree_copies + last_copies:
         made.wait_send()
-
-
-def scattered(wide, grad_down, grad_up, collective_id=1):
+    for made in swaps:
+        made.wait()
+    stay.wait()
+
+
+def scattered(wide, grad_down, grad_up, slot_grad, forward, collective_id=1):
     _, rows, rank = grad_down.shape
     half = rank // 2
     slots = len(tree_slots(wide))
     vmem = pl.BlockSpec(memory_space=pltpu.VMEM)
+    hbm = pl.BlockSpec(memory_space=pl.ANY)
     held = jnp.bfloat16
+    slots_all, samples = slot_grad.shape[:2]
     return pl.pallas_call(
         functools.partial(scatter_kernel, wide),
         out_shape=(
             jax.ShapeDtypeStruct((rows, rank), jnp.float32),
             jax.ShapeDtypeStruct((rows, rank), jnp.float32),
-        ),
-        in_specs=[vmem, vmem],
-        out_specs=(vmem, vmem),
+            jax.ShapeDtypeStruct((slots_all // wide, wide) + slot_grad.shape[1:], held),
+            jax.ShapeDtypeStruct((samples, wide * rows), held),
+        ),
+        in_specs=[vmem, vmem, hbm, pl.BlockSpec(memory_space=pltpu.SMEM)] + [vmem] * 6,
+        out_specs=(vmem, vmem, hbm, vmem),
         scratch_shapes=[
+            pltpu.VMEM((samples, wide * rows), held),
+            pltpu.VMEM((samples, rank), jnp.float32),
             pltpu.VMEM((2, wide // 2, rows, rank), held),
             pltpu.VMEM((2, wide // 2, rows, half), held),
             pltpu.VMEM((2, wide // 2, rows, half), held),
@@ -328,35 +389,171 @@
             pltpu.SemaphoreType.DMA((2, wide)),
             pltpu.SemaphoreType.DMA((2, 2 * slots)),
             pltpu.SemaphoreType.DMA((2, 2)),
+            pltpu.SemaphoreType.DMA((2, wide)),
         ],
         compiler_params=pltpu.CompilerParams(
             collective_id=collective_id, has_side_effects=True,
-            vmem_limit_bytes=40 * 1024 * 1024,
+            vmem_limit_bytes=VMEM_LIMIT,
         ),
         cost_estimate=pl.CostEstimate(
             flops=0, bytes_accessed=wide * rows * rank * 40, transcendentals=0
         ),
         name="gradients_scatter",
-    )(grad_down, grad_up)
-
-
-def table_means(slot_rows, lookup_count, table_slots):
-    picked = jnp.take(slot_rows, table_slots, axis=0).astype(jnp.float32)
-    scaled = picked / jnp.transpose(lookup_count).astype(jnp.float32)[:, :, None]
-    return jnp.transpose(scaled, (1, 0, 2)).reshape(scaled.shape[1], -1).astype(jnp.bfloat16)
+    )(grad_down, grad_up, slot_grad, *forward)
 
 
 OVER_ROWS = (((0,), (0,)), ((), ()))
 OVER_COLS = (((1,), (1,)), ((), ()))
-
-
-def dot(left, right, dims):
+PLAIN = (((1,), (0,)), ((), ()))
+VMEM_LIMIT = 60 * 1024 * 1024
+
+
+def dot(left, right, dims=PLAIN):
     return lax.dot_general(left, right, dims, preferred_element_type=jnp.float32)
 
 
-def cross_forward(stacked, down, up_rows):
-    low_rank = jnp.dot(stacked, down, preferred_element_type=jnp.float32).astype(jnp.bfloat16)
-    return low_rank, dot(low_rank, up_rows, OVER_COLS)
+def group_of(features):
+    return next(size for size in (3, 2, 1) if features % size == 0)
+
+
+def spread_counts(counts, step, group, feature):
+    lanes = counts.shape[1]
+    row = lax.broadcasted_iota(jnp.int32, (lanes, feature), 0)
+    pieces = []
+    for part in range(group):
+        pick = (row == step * group + part).astype(jnp.float32).astype(jnp.bfloat16)
+        pieces.append(dot(counts, pick))
+    return pieces
+
+
+def forward_b(
+    slot_ref, arrived_ref, dense_ref, counts_ref, down_ref, up_ref, bias_ref,
+    crossed_out, stacked_held, low_held,
+):
+    samples, feature = dense_ref.shape
+    features = down_ref.shape[0] // feature
+    group = group_of(features)
+    span = group * feature
+    low_held[...] = jnp.zeros_like(low_held)
+
+    def first(step, carry):
+        divisors = spread_counts(counts_ref[...], step, group, feature)
+        pieces = []
+        for part in range(group):
+            table = jnp.maximum(step * group + part - 1, 0)
+            rows = arrived_ref[slot_ref[table]].astype(jnp.float32)
+            if part == 0:
+                rows = jnp.where(step == 0, dense_ref[...].astype(jnp.float32), rows)
+            pieces.append((rows / divisors[part]).astype(jnp.bfloat16))
+        stacked = jnp.concatenate(pieces, axis=1)
+        columns = pl.ds(pl.multiple_of(step * span, span), span)
+        stacked_held[:, columns] = stacked
+        low_held[...] += dot(stacked, down_ref[columns, :])
+        return carry
+
+    lax.fori_loop(0, features // group, first, 0)
+    low = low_held[...].astype(jnp.bfloat16)
+
+    def second(step, carry):
+        columns = pl.ds(pl.multiple_of(step * span, span), span)
+        projected = dot(low, up_ref[columns, :], OVER_COLS)
+        wide_b = stacked_held[:, columns].astype(jnp.float32)
+        crossed = wide_b * (projected + bias_ref[:, columns]) + wide_b
+        crossed_out[:, columns] = crossed.astype(jnp.bfloat16)
+        return carry
+
+    lax.fori_loop(0, features // group, second, 0)
+
+
+def backward_kernel(
+    slot_ref, stacked_ref, upstream_ref, counts_ref, down_ref, up_ref, bias_ref,
+    dense_out, slot_out, grad_down_out, grad_up_out, low_held, low_grad_held,
+):
+    feature = dense_out.shape[1]
+    features = down_ref.shape[0] // feature
+    group = group_of(features)
+    span = group * feature
+    low_held[...] = jnp.zeros_like(low_held)
+    low_grad_held[...] = jnp.zeros_like(low_grad_held)
+
+    def scaled(columns):
+        upstream = upstream_ref[:, columns].astype(jnp.float32)
+        return (upstream * stacked_ref[:, columns].astype(jnp.float32)).astype(jnp.bfloat16)
+
+    def first(step, carry):
+        columns = pl.ds(pl.multiple_of(step * span, span), span)
+        low_held[...] += dot(stacked_ref[:, columns], down_ref[columns, :])
+        low_grad_held[...] += dot(scaled(columns), up_ref[columns, :])
+        return carry
+
+    lax.fori_loop(0, features // group, first, 0)
+    low = low_held[...].astype(jnp.bfloat16)
+    low_grad = low_grad_held[...].astype(jnp.bfloat16)
+    for table in range(features - 1, slot_ref.shape[0]):
+        slot_out[slot_ref[table]] = jnp.zeros(slot_out.shape[1:], slot_out.dtype)
+
+    def second(step, carry):
+        columns = pl.ds(pl.multiple_of(step * span, span), span)
+        grad_down_out[columns, :] = dot(
+            stacked_ref[:, columns], low_grad, OVER_ROWS
+        ).astype(jnp.bfloat16)
+        grad_up_out[columns, :] = dot(scaled(columns), low, OVER_ROWS).astype(jnp.bfloat16)
+        upstream = upstream_ref[:, columns].astype(jnp.float32)
+        projected = dot(low, up_ref[columns, :], OVER_COLS)
+        grad = upstream * (projected + bias_ref[:, columns]) + upstream
+        grad = grad + dot(low_grad, down_ref[columns, :], OVER_COLS)
+        divisors = spread_counts(counts_ref[...], step, group, feature)
+        for part in range(group):
+            block = grad[:, part * feature : (part + 1) * feature] / divisors[part]
+            block = block.astype(jnp.bfloat16)
+            number = step * group + part
+            if part:
+                slot_out[slot_ref[number - 1]] = block
+            else:
+
+                @pl.when(step == 0)
+                def _():
+                    dense_out[...] = block
+
+                @pl.when(step > 0)
+                def _():
+                    slot_out[slot_ref[number - 1]] = block
+
+        return carry
+
+    lax.fori_loop(0, features // group, second, 0)
+
+
+def backward(slot_of, stacked, upstream, counts, down, up_rows, bias, feature):
+    samples, width = stacked.shape
+    rank = down.shape[1]
+    held = jnp.bfloat16
+    vmem = pl.BlockSpec(memory_space=pltpu.VMEM)
+    return pl.pallas_call(
+        backward_kernel,
+        out_shape=(
+            jax.ShapeDtypeStruct((samples, feature), held),
+            jax.ShapeDtypeStruct((slot_of.shape[0], samples, feature), held),
+            jax.ShapeDtypeStruct((width, rank), held),
+            jax.ShapeDtypeStruct((width, rank), held),
+        ),
+        in_specs=[pl.BlockSpec(memory_space=pltpu.SMEM)] + [vmem] * 6,
+        out_specs=(vmem,) * 4,
+        scratch_shapes=[
+            pltpu.VMEM((samples, rank), jnp.float32),
+            pltpu.VMEM((samples, rank), jnp.float32),
+        ],
+        compiler_params=pltpu.CompilerParams(vmem_limit_bytes=VMEM_LIMIT),
+        cost_estimate=pl.CostEstimate(
+            flops=12 * samples * width * rank, bytes_accessed=20 << 20, transcendentals=0
+        ),
+        name="cross_backward",
+    )(slot_of, stacked, upstream, counts, down, up_rows, bias)
+
+
+def divisors_of(counts):
+    held = jnp.pad(counts.astype(jnp.bfloat16), ((0, 0), (1, 0)), constant_values=1)
+    return jnp.pad(held, ((0, 0), (0, -held.shape[1] % 128)))
 
 
 def local(
@@ -373,12 +570,9 @@
     cross_layer_bias,
 ):
     feature = dense_output_second.shape[1]
-    tables = counts_b.shape[1]
-    table_slots = slot_of[:tables]
     shard = down_projection.shape[0]
     rank = down_projection.shape[1]
     width = stacked_a.shape[1]
-    samples = stacked_a.shape[0]
     me = lax.axis_index("wide")
     lanes = -(-shard // 128) * 128
 
@@ -389,55 +583,24 @@
     holds = (jnp.arange(wide) == me) & (lax.axis_index("pair") == 0)
     bias_own = jnp.where(holds[:, None], cross_layer_bias.astype(jnp.float32)[None, :], 0.0)
     vec = jnp.pad(jnp.concatenate([bias_share, bias_own], axis=0), ((0, 0), (0, lanes - shard)))
-    down_all, up_all, vec_all = gathered(wide, down_projection, jnp.transpose(proj_up), vec)
+    down_all, up_all, vec_all, arrived = gathered(
+        wide, down_projection, jnp.transpose(proj_up), vec, pooled_b
+    )
     grad_bias = lax.dynamic_index_in_dim(vec_all, me, 0, keepdims=False)[:shard]
-    bias = vec_all[wide:, :shard].reshape(width)
-
-    pooled_b, down_all = lax.optimization_barrier((pooled_b, down_all))
-    arrived = lax.all_to_all(pooled_b, "wide", split_axis=1, concat_axis=0, tiled=True)
-    slot_count = arrived.shape[0]
-
+    bias = vec_all[wide:, :shard].reshape(1, width)
     down = down_all.reshape(width, rank)
     up_rows = up_all.reshape(width, rank)
 
-    proj_grad = scale_grad.astype(jnp.bfloat16)
-    low_grad = jnp.dot(proj_grad, up_rows, preferred_element_type=jnp.float32).astype(jnp.bfloat16)
-    low_a, projected = cross_forward(stacked_a, down, up_rows)
-    input_grad = upstream_wide * (projected + bias) + upstream_wide
-    input_grad = input_grad + dot(low_grad, down, OVER_COLS)
-    grad_down = dot(stacked_a, low_grad, OVER_ROWS).astype(jnp.bfloat16)
-    grad_up = dot(proj_grad, low_a, OVER_ROWS).astype(jnp.bfloat16)
-    dense_gradient = input_grad[:, :feature].astype(jnp.bfloat16)
-    table_gradient = (
-        input_grad[:, feature:].reshape(samples, -1, feature)
-        / counts_a.astype(jnp.float32)[:, :, None]
+    dense_gradient, slot_grad, grad_down, grad_up = backward(
+        slot_of, stacked_a, upstream_a, divisors_of(counts_a), down, up_rows, bias, feature
     )
-    table_gradient = jnp.transpose(table_gradient, (1, 0, 2)).astype(jnp.bfloat16)
-    slot_selector = (
-        table_slots[None, :] == jnp.arange(slot_count, dtype=jnp.int32)[:, None]
-    ).astype(jnp.bfloat16)
-    slot_grad = jnp.einsum(
-        "qv,vxk->qxk", slot_selector, table_gradient, preferred_element_type=jnp.float32
-    ).astype(jnp.bfloat16)
-    slot_grad, grad_down, grad_up = lax.optimization_barrier((slot_grad, grad_down, grad_up))
-    returned = lax.all_to_all(
-        slot_grad.reshape(slot_count, 1, samples, feature),
-        "wide",
-        split_axis=0,
-        concat_axis=1,
-        tiled=True,
+    down_sum, up_sum, returned, crossed_b = scattered(
+        wide,
+        grad_down.reshape(wide, shard, rank),
+        grad_up.reshape(wide, shard, rank),
+        slot_grad,
+        (slot_of, arrived, dense_output_second, divisors_of(counts_b), down, up_rows, bias),
     )
-    down_sum, up_sum = scattered(
-        wide, grad_down.reshape(wide, shard, rank), grad_up.reshape(wide, shard, rank)
-    )
-
-    slot_rows = arrived.reshape(slot_count, samples, feature)
-    stacked_b = jnp.concatenate(
-        [dense_output_second, table_means(slot_rows, counts_b, table_slots)], axis=1
-    )
-    _, projected_b = cross_forward(stacked_b, down, up_rows)
-    b_wide = stacked_b.astype(jnp.float32)
-    crossed_b = (b_wide * (projected_b + bias) + b_wide).astype(jnp.bfloat16)
     return (crossed_b, dense_gradient, returned, down_sum, jnp.transpose(up_sum), grad_bias)
 
 

time: 209 us -> 190 us (0.909)
  Pallas kernels: 110 us -> 173 us
  local copies, waits for them, and re-layouts: 43 us -> 8.87 us
  matrix products: 19.8 us -> 0 us
  starting transfers between devices: 17.2 us -> 0 us
  waiting for transfers between devices: 6.48 us -> 0 us
  other arithmetic: 10.9 us -> 6.83 us
    pallas_call x1, Pallas kernels: 54.4 us -> 77.3 us  [scattered(): pl.pallas_call(functools.partial(scatter_kernel, wide), out_shape=(jax.Sh...]
    pallas_call x1, Pallas kernels: 55.4 us -> 76.8 us  [gathered(): pl.pallas_call(functools.partial(gather_kernel, wide), out_shape=(jax.Sha...]
    dot_general x8 -> x0, matrix products: 19.8 us -> none  [the longest x5 13 us: dot(): lax.dot_general(left, right, dims, preferred_element_type=jnp.float32)]
    pallas_call x0 -> x1, Pallas kernels: none -> 19 us  [backward(): pl.pallas_call(backward_kernel, out_shape=(jax.ShapeDtypeStruct((samples,...]
    all_to_all x2 -> x0, starting transfers between devices: 17.2 us -> none  [the longest x1 11.3 us: local(): lax.all_to_all(slot_grad.reshape(slot_count, 1, samples, feature), 'wide'...]
    slice x4 -> x1, local copies, waits for them, and re-layouts: 9.84 us -> 0.72 us  [local(): bias = vec_all[wide:, :shard].reshape(1, width)]
    optimization_barrier x2 -> x0, local copies, waits for them, and re-layouts: 9.02 us -> none  [the longest x1 5.76 us: local(): lax.optimization_barrier((slot_grad, grad_down, grad_up))]
    all_to_all x2 -> x0, waiting for transfers between devices: 6.48 us -> none  [the longest x1 6.47 us: local(): lax.all_to_all(pooled_b, 'wide', split_axis=1, concat_axis=0, tiled=True)]
  transfers between devices with their start and end apart: 2 -> 0, of which waited for: 1 -> 0; matrix products, arithmetic and copies ran while one was open for 24% -> 0% of each run, Pallas kernels for 26% -> 0%
where the time goes in v2:
time: 190 us
  Pallas kernels  173 us (91%)
  local copies, waits for them, and re-layouts  8.87 us (5%)
  other arithmetic  6.83 us (4%)
    pallas_call x1, Pallas kernels, scattered(): pl.pallas_call(functools.partial(scatter_kernel, wide), out_shape=(jax.Sh...  77.3 us
    pallas_call x1, Pallas kernels, gathered(): pl.pallas_call(functools.partial(gather_kernel, wide), out_shape=(jax.Sha...  76.8 us
    pallas_call x1, Pallas kernels, backward(): pl.pallas_call(backward_kernel, out_shape=(jax.ShapeDtypeStruct((samples,...  19 us
    unnamed x10, local copies, waits for them, and re-layouts  5.81 us

profile of v2, /device:TPU:0, one launch (start us, length us, event | category | flops | bytes accessed | tf_op | source)
XLA Modules:
  0.0 189.5 jit_solution(15424798655078065422)
XLA Ops:
  0.7 0.7 convert_element_type.26
  1.3 0.1 broadcast_select_fusion
  1.4 0.8 convert_element_type.27
  2.1 0.8 convert_element_type.23
  2.9 2.5 %multiply_reduce_fusion = f32[3456]{0:T(1024)S(1)} fusion(bf16[256,3456]{1,0:T(8,128)(2,1)} %stacked_ref.1, bf16[256,3456]{1,0:T(8,128)(2,1)} %upstream_ref.1), kind=kLoop, calls=%fused_computation | loop fusion | flops 3535488 | bytes 3552768 | tf_op jit(solution)/shard_map/reduce_sum | solution.py:582
  5.4 0.1 reshape.37
  5.5 0.6 select_maximum_fusion.vec_ref
  6.1 0.1 copy.18
  6.3 0.7 fusion.1.counts_ref
  7.0 0.1 copy.19
  7.1 0.7 fusion.counts_ref
  7.8 76.8 %weights_gather.1 = (bf16[16,216,512]{2,1,0:T(8,128)(2,1)}, bf16[16,216,512]{2,1,0:T(8,128)(2,1)}, f32[32,256]{1,0:T(8,128)}, bf16[32,256,128]{2,1,0:T(8,128)(2,1)}) custom-call(bf16[216,512]{1,0:T(8,128)(2,1)} %down_ref.1, bf16[216,512]{1,0:T(8,128)(2,1)} %bitcast.14, f32[32,256]{1,0:T(8,128)} %select_maximum_fusion.vec_ref, ...), custom_call_target="tpu_custom_call" | custom-call | bytes 70778880 | tf_op jit(solution)/shard_map/weights_gather/pallas_call | solution.py:187
  84.7 1.3 constant_dynamic-slice_fusion
  85.9 0.7 slice.9
  86.7 0.7 reshape.40.bias_ref
  87.4 19.0 %cross_backward.1 = (bf16[256,128]{1,0:T(8,128)(2,1)}, bf16[32,256,128]{2,1,0:T(8,128)(2,1)}, bf16[3456,512]{1,0:T(8,128)(2,1)}, bf16[3456,512]{1,0:T(8,128)(2,1)}) custom-call(s32[32]{0:T(128)} %slot_ref.3, bf16[256,3456]{1,0:T(8,128)(2,1)} %stacked_ref.1, bf16[256,3456]{1,0:T(8,128)(2,1)} %upstream_ref.1, bf16[256,128]{1,0:T(8,128)(2,1)} %fusion.1.counts_ref, ...), custom_call_target="tpu_custom_call" | custom-call | flops 5435817984 | bytes 20971520 | tf_op jit(solution)/shard_map/cross_backward/pallas_call | solution.py:532
  106.3 77.3 %gradients_scatter.1 = (f32[216,512]{1,0:T(8,128)}, f32[216,512]{1,0:T(8,128)}, bf16[2,16,256,128]{3,2,1,0:T(8,128)(2,1)}, bf16[256,3456]{1,0:T(8,128)(2,1)}) custom-call(bf16[16,216,512]{2,1,0:T(8,128)(2,1)} %bitcast.11, bf16[16,216,512]{2,1,0:T(8,128)(2,1)} %bitcast.12, bf16[32,256,128]{2,1,0:T(8,128)(2,1)} %get-tuple-element.23.slot_grad_ref, ...), custom_call_target="tpu_custom_call" | custom-call | bytes 70778880 | tf_op jit(solution)/shard_map/gradients_scatter/pallas_call | solution.py:368
  183.7 0.0 copy-start
  183.7 3.0 %copy.24 = bf16[256,3456]{1,0:T(8,128)(2,1)} copy(bf16[256,3456]{1,0:T(8,128)(2,1)} %get-tuple-element.36) | data formatting | bytes 3538944
  186.7 0.0 copy-done
  186.7 0.0 copy-start.2
  186.7 0.0 copy-start.1
  186.7 1.3 copy.25
  188.0 0.0 copy-done.2
  188.0 0.8 copy.26
  188.7 0.0 copy-done.1
  188.7 0.8 copy.27
  (1 shorter events, 0.0 us)
Async XLA Ops:
  183.7 3.0 %copy-start = (bf16[2,16,256,128]{3,2,1,0:T(8,128)(2,1)S(1)}, bf16[2,16,256,128]{3,2,1,0:T(8,128)(2,1)}, u32[]{:S(2)}) copy-start(bf16[2,16,256,128]{3,2,1,0:T(8,128)(2,1)} %get-tuple-element.38) | copy-start | bytes 6291460
  186.7 1.3 copy-start.2
  186.7 2.1 %copy-start.1 = (f32[216,512]{1,0:T(8,128)S(1)}, f32[216,512]{1,0:T(8,128)}, u32[]{:S(2)}) copy-start(f32[216,512]{1,0:T(8,128)} %get-tuple-element.29) | copy-start | bytes 1327108

commit v3 on v2

--- a/solution.py
+++ b/solution.py
@@ -39,23 +39,40 @@
     pl.semaphore_wait(barrier, wide)
 
 
-def exchange(wide, me, source, target, sems):
-    copies = []
-    for offset in range(wide - 1, 0, -1):
-        peer = flipped(me, offset)
-        made = pltpu.make_async_remote_copy(
-            src_ref=source(peer),
-            dst_ref=target(me),
-            send_sem=sems.at[0, offset],
-            recv_sem=sems.at[1, offset],
-            device_id={"wide": peer},
-            device_id_type=MESH,
-        )
-        made.start()
-        copies.append(made)
-    keep = pltpu.make_async_copy(source(me), target(me), sems.at[0, 0])
-    keep.start()
-    return copies, keep
+class Exchange:
+    def __init__(self, wide, me, source, target, sems):
+        self.me, self.source, self.target, self.sems = me, source, target, sems
+        offsets = range(wide - 1, 0, -1)
+        self.plain = [offset for offset in offsets if not offset & 2]
+        self.crossing = [offset for offset in offsets if offset & 2]
+        self.copies = []
+        self.keep = pltpu.make_async_copy(source(me), target(me), sems.at[0, 0])
+        self.keep.start()
+
+    def send(self, waiting, count):
+        for offset in waiting[:count]:
+            peer = flipped(self.me, offset)
+            made = pltpu.make_async_remote_copy(
+                src_ref=self.source(peer),
+                dst_ref=self.target(self.me),
+                send_sem=self.sems.at[0, offset],
+                recv_sem=self.sems.at[1, offset],
+                device_id={"wide": peer},
+                device_id_type=MESH,
+            )
+            made.start()
+            self.copies.append(made)
+        del waiting[:count]
+
+    def send_rest(self):
+        self.send(self.plain, len(self.plain))
+        self.send(self.crossing, len(self.crossing))
+
+    def finish(self):
+        self.send_rest()
+        self.keep.wait()
+        for made in self.copies:
+            made.wait()
 
 
 def gather_kernel(
@@ -138,17 +155,19 @@
         own.append(keep)
 
     each = pooled_ref.shape[0]
-    swaps = None
+    swap = Exchange(
+        wide,
+        me,
+        lambda peer: pooled_ref.at[:, peer],
+        lambda owner: arrived_out.at[pl.ds(owner * each, each)],
+        swap_sems,
+    )
     known = [0]
     for position, stage in enumerate(stages):
-        if swaps is None and (stage[0] == "pair" or stage[1] == 2):
-            swaps, stay = exchange(
-                wide,
-                me,
-                lambda peer: pooled_ref.at[:, peer],
-                lambda owner: arrived_out.at[pl.ds(owner * each, each)],
-                swap_sems,
-            )
+        if stage[0] == "wide" and stage[1] > 2:
+            swap.send(swap.plain, 2)
+        else:
+            swap.send_rest()
         if stage[0] == "pair":
             for offset in known[1:]:
                 await_block(offset, 1)
@@ -170,10 +189,9 @@
             vectors[position + 1].start()
         else:
             vec_out[...] = total
-    for keep in own + [stay]:
+    for keep in own:
         keep.wait()
-    for made in swaps:
-        made.wait()
+    swap.finish()
     for made in sends + vectors:
         made.wait_send()
 
@@ -277,13 +295,14 @@
                 core_copies[(part, offset, kind)] = made
 
     each = returned_out.shape[0]
-    swaps, stay = exchange(
+    swap = Exchange(
         wide,
         me,
         lambda peer: slot_grad_ref.at[pl.ds(peer * each, each)],
         lambda owner: returned_out.at[:, owner],
         swap_sems,
     )
+    swap.send(swap.plain, wide)
 
     def both_cores(kind, offset, columns):
         own = ins[kind][flipped(me, offset), :, columns].astype(jnp.float32)
@@ -304,14 +323,17 @@
             made.start()
             pair_copies[(offset, kind)] = made
 
-    forward_b(
-        slot_ref, arrived_ref, dense_ref, counts_ref, weight_down_ref, weight_up_ref, bias_ref,
-        crossed_out, stacked_held, low_held,
+    forward_low(
+        slot_ref, arrived_ref, dense_ref, counts_ref, weight_down_ref, stacked_held, low_held
     )
 
     tree_copies = []
     last_copies = []
     for offset in order:
+        if swap.crossing and not offset & 2:
+            swap.send_rest()
+        if offset == order[len(order) // 2]:
+            forward_out(weight_up_ref, bias_ref, crossed_out, stacked_held, low_held)
         for kind in range(2):
             core_copies[(0, offset, kind)].wait_recv()
             pair_copies[(offset, kind)].wait_recv()
@@ -336,6 +358,7 @@
                 )
                 made.start()
                 tree_copies.append(made)
+                swap.send(swap.crossing, 1)
             else:
                 rounded = total.astype(jnp.bfloat16)
                 last_send[kind] = rounded
@@ -352,9 +375,7 @@
         made.wait_send()
     for made in tree_copies + last_copies:
         made.wait_send()
-    for made in swaps:
-        made.wait()
-    stay.wait()
+    swap.finish()
 
 
 def scattered(wide, grad_down, grad_up, slot_grad, forward, collective_id=1):
@@ -426,9 +447,8 @@
     return pieces
 
 
-def forward_b(
-    slot_ref, arrived_ref, dense_ref, counts_ref, down_ref, up_ref, bias_ref,
-    crossed_out, stacked_held, low_held,
+def forward_low(
+    slot_ref, arrived_ref, dense_ref, counts_ref, down_ref, stacked_held, low_held
 ):
     samples, feature = dense_ref.shape
     features = down_ref.shape[0] // feature
@@ -452,6 +472,11 @@
         return carry
 
     lax.fori_loop(0, features // group, first, 0)
+
+
+def forward_out(up_ref, bias_ref, crossed_out, stacked_held, low_held):
+    width = up_ref.shape[0]
+    span = 128 * group_of(width // 128)
     low = low_held[...].astype(jnp.bfloat16)
 
     def second(step, carry):
@@ -462,7 +487,7 @@
         crossed_out[:, columns] = crossed.astype(jnp.bfloat16)
         return carry
 
-    lax.fori_loop(0, features // group, second, 0)
+    lax.fori_loop(0, width // span, second, 0)
 
 
 def backward_kernel(

time: 190 us -> 182 us (0.958)
  Pallas kernels: 173 us -> 165 us
    pallas_call x1, Pallas kernels: 76.8 us -> 70.8 us  [gathered(): pl.pallas_call(functools.partial(gather_kernel, wide), out_shape=(jax.Sha...]
where the time goes in v3:
time: 182 us
  Pallas kernels  165 us (91%)
  local copies, waits for them, and re-layouts  8.87 us (5%)
  other arithmetic  6.83 us (4%)
    pallas_call x1, Pallas kernels, scattered(): pl.pallas_call(functools.partial(scatter_kernel, wide), out_shape=(jax.Sh...  75.7 us
    pallas_call x1, Pallas kernels, gathered(): pl.pallas_call(functools.partial(gather_kernel, wide), out_shape=(jax.Sha...  70.8 us
    pallas_call x1, Pallas kernels, backward(): pl.pallas_call(backward_kernel, out_shape=(jax.ShapeDtypeStruct((samples,...  19 us
    unnamed x10, local copies, waits for them, and re-layouts  5.81 us

profile of v3, /device:TPU:0, one launch (start us, length us, event | category | flops | bytes accessed | tf_op | source)
XLA Modules:
  0.0 181.8 jit_solution(9122896901801016926)
XLA Ops:
  0.7 0.7 convert_element_type.26
  1.3 0.1 broadcast_select_fusion
  1.4 0.8 convert_element_type.27
  2.1 0.8 convert_element_type.23
  2.9 2.5 %multiply_reduce_fusion = f32[3456]{0:T(1024)S(1)} fusion(bf16[256,3456]{1,0:T(8,128)(2,1)} %stacked_ref.1, bf16[256,3456]{1,0:T(8,128)(2,1)} %upstream_ref.1), kind=kLoop, calls=%fused_computation | loop fusion | flops 3535488 | bytes 3552768 | tf_op jit(solution)/shard_map/reduce_sum | solution.py:607
  5.4 0.1 reshape.37
  5.5 0.6 select_maximum_fusion.vec_ref
  6.1 0.1 copy.18
  6.3 0.7 fusion.1.counts_ref
  7.0 0.1 copy.19
  7.1 0.7 fusion.counts_ref
  7.8 70.8 %weights_gather.1 = (bf16[16,216,512]{2,1,0:T(8,128)(2,1)}, bf16[16,216,512]{2,1,0:T(8,128)(2,1)}, f32[32,256]{1,0:T(8,128)}, bf16[32,256,128]{2,1,0:T(8,128)(2,1)}) custom-call(bf16[216,512]{1,0:T(8,128)(2,1)} %down_ref.1, bf16[216,512]{1,0:T(8,128)(2,1)} %bitcast.14, f32[32,256]{1,0:T(8,128)} %select_maximum_fusion.vec_ref, ...), custom_call_target="tpu_custom_call" | custom-call | bytes 70778880 | tf_op jit(solution)/shard_map/weights_gather/pallas_call | solution.py:205
  78.6 1.3 constant_dynamic-slice_fusion
  79.9 0.7 slice.9
  80.6 0.7 reshape.40.bias_ref
  81.3 19.0 %cross_backward.1 = (bf16[256,128]{1,0:T(8,128)(2,1)}, bf16[32,256,128]{2,1,0:T(8,128)(2,1)}, bf16[3456,512]{1,0:T(8,128)(2,1)}, bf16[3456,512]{1,0:T(8,128)(2,1)}) custom-call(s32[32]{0:T(128)} %slot_ref.3, bf16[256,3456]{1,0:T(8,128)(2,1)} %stacked_ref.1, bf16[256,3456]{1,0:T(8,128)(2,1)} %upstream_ref.1, bf16[256,128]{1,0:T(8,128)(2,1)} %fusion.1.counts_ref, ...), custom_call_target="tpu_custom_call" | custom-call | flops 5435817984 | bytes 20971520 | tf_op jit(solution)/shard_map/cross_backward/pallas_call | solution.py:557
  100.3 75.7 %gradients_scatter.1 = (f32[216,512]{1,0:T(8,128)}, f32[216,512]{1,0:T(8,128)}, bf16[2,16,256,128]{3,2,1,0:T(8,128)(2,1)}, bf16[256,3456]{1,0:T(8,128)(2,1)}) custom-call(bf16[16,216,512]{2,1,0:T(8,128)(2,1)} %bitcast.11, bf16[16,216,512]{2,1,0:T(8,128)(2,1)} %bitcast.12, bf16[32,256,128]{2,1,0:T(8,128)(2,1)} %get-tuple-element.23.slot_grad_ref, ...), custom_call_target="tpu_custom_call" | custom-call | bytes 70778880 | tf_op jit(solution)/shard_map/gradients_scatter/pallas_call | solution.py:389
  176.0 0.0 copy-start
  176.0 3.0 %copy.24 = bf16[256,3456]{1,0:T(8,128)(2,1)} copy(bf16[256,3456]{1,0:T(8,128)(2,1)} %get-tuple-element.36) | data formatting | bytes 3538944
  179.0 0.0 copy-done
  179.0 0.0 copy-start.2
  179.0 0.0 copy-start.1
  179.0 1.3 copy.25
  180.3 0.0 copy-done.2
  180.3 0.8 copy.26
  181.1 0.0 copy-done.1
  181.1 0.8 copy.27
  (1 shorter events, 0.0 us)
Async XLA Ops:
  176.0 3.0 %copy-start = (bf16[2,16,256,128]{3,2,1,0:T(8,128)(2,1)S(1)}, bf16[2,16,256,128]{3,2,1,0:T(8,128)(2,1)}, u32[]{:S(2)}) copy-start(bf16[2,16,256,128]{3,2,1,0:T(8,128)(2,1)} %get-tuple-element.38) | copy-start | bytes 6291460
  179.0 1.3 copy-start.2
  179.0 2.1 %copy-start.1 = (f32[216,512]{1,0:T(8,128)S(1)}, f32[216,512]{1,0:T(8,128)}, u32[]{:S(2)}) copy-start(f32[216,512]{1,0:T(8,128)} %get-tuple-element.29) | copy-start | bytes 1327108
